TPU v7x, 32 devices: a whole 2x2x4 slice. The times are simulated.
32 devices in a mesh: seq: 4 (over z), shard: 8 (over y, x, core).
Axes of the slice: x: 2, y: 2, z: 4, core: 2. Of those that a mesh axis runs over, the one named last changes fastest.
Arguments:
- tokens: bfloat16 [8, 2048, 1024], P('shard', 'seq'), may hold values from -6 to 6
- ln1_gain: bfloat16 [1024], P(('seq', 'shard')), may hold values from 0.5 to 1.5
- ln1_bias: bfloat16 [1024], P(('seq', 'shard')), may hold values from -3 to 3
- w_qkv: bfloat16 [1024, 3072], P(('seq', 'shard')), may hold values from -0.1875 to 0.1875
- bias_query: bfloat16 [1024], P(('seq', 'shard')), may hold values from -3 to 3
- bias_value: bfloat16 [1024], P(('seq', 'shard')), may hold values from -3 to 3
- w_out: bfloat16 [1024, 1024], P(('seq', 'shard')), may hold values from -1 to 1
- bias_out: bfloat16 [1024], P(('seq', 'shard')), may hold values from -3 to 3
- ln2_gain: bfloat16 [1024], P(('seq', 'shard')), may hold values from 0.5 to 1.5
- ln2_bias: bfloat16 [1024], P(('seq', 'shard')), may hold values from -3 to 3
- w_in: bfloat16 [1024, 4096], P(('seq', 'shard')), may hold values from -0.1875 to 0.1875
- bias_in: bfloat16 [4096], P(('seq', 'shard')), may hold values from -3 to 3
- w_back: bfloat16 [4096, 1024], P(('seq', 'shard')), may hold values from -0.09375 to 0.09375
- bias_back: bfloat16 [1024], P(('seq', 'shard')), may hold values from -3 to 3
- cotangent: bfloat16 [8, 2048, 1024], P('shard', 'seq'), may hold values from -6 to 6
Outputs:
- result: bfloat16 [8, 2048, 1024], P('shard', 'seq')
- grad_tokens: float32 [8, 2048, 1024], P('shard', 'seq')
- grad_ln1_gain: float32 [1024], P(('seq', 'shard'))
- grad_ln1_bias: float32 [1024], P(('seq', 'shard'))
- grad_w_qkv: float32 [1024, 3072], P(('seq', 'shard'))
- grad_bias_query: float32 [1024], P(('seq', 'shard'))
- grad_bias_value: float32 [1024], P(('seq', 'shard'))
- grad_w_out: float32 [1024, 1024], P(('seq', 'shard'))
- grad_bias_out: float32 [1024], P(('seq', 'shard'))
- grad_ln2_gain: float32 [1024], P(('seq', 'shard'))
- grad_ln2_bias: float32 [1024], P(('seq', 'shard'))
- grad_w_in: float32 [1024, 4096], P(('seq', 'shard'))
- grad_bias_in: float32 [4096], P(('seq', 'shard'))
- grad_w_back: float32 [4096, 1024], P(('seq', 'shard'))
- grad_bias_back: float32 [1024], P(('seq', 'shard'))
All inputs are finite; a program needn't handle non-finite values.
Results may differ from a plain program's by a relative error of at most 0.014.
The roundings to bfloat16 on the way count: a program that leaves them out, or rounds other values in their place, can miss the bound.
Values may be sent and summed in bfloat16 or wider, within the bound.
A program may use at most 192 MiB of HBM per device.

v0:
```python
import math
import jax
import jax.numpy as jnp
from jax import lax
from jax.sharding import PartitionSpec as P

HEAD_DIM = 64
norm_eps = 1e-05
gelu_c = math.sqrt(2.0 / math.pi)


def normalize(values):
    mean_row = jnp.mean(values, axis=-1, keepdims=True)
    centred = values - mean_row
    var_row = jnp.mean(centred * centred, axis=-1, keepdims=True)
    scale_row = lax.rsqrt(var_row + norm_eps)
    return (centred * scale_row, scale_row)


def norm_back(dnormed, normed, scale_row):
    return scale_row * (
        dnormed
        - jnp.mean(dnormed, axis=-1, keepdims=True)
        - normed * jnp.mean(dnormed * normed, axis=-1, keepdims=True)
    )


def gelu_pair(inputs):
    inner = gelu_c * (inputs + 0.044715 * inputs * inputs * inputs)
    tanh_val = jnp.tanh(inner)
    value = 0.5 * inputs * (1.0 + tanh_val)
    slope = 0.5 * (1.0 + tanh_val) + 0.5 * inputs * (1.0 - tanh_val * tanh_val) * gelu_c * (
        1.0 + 3.0 * 0.044715 * inputs * inputs
    )
    return (value, slope)


def masked_scores(query_block, keys, start, scale):
    block = query_block.shape[0]
    length = keys.shape[0]
    scores = (
        jnp.einsum("qgd,kgd->gqk", query_block, keys, preferred_element_type=jnp.float32) * scale
    )
    q_pos = start + jnp.arange(block, dtype=jnp.int32)
    k_pos = jnp.arange(length, dtype=jnp.int32)
    allowed = k_pos[None, None, :] <= q_pos[None, :, None]
    return jnp.where(allowed, scores, -1e30)


def attend_forward(query, keys, values):
    length, groups, width = query.shape
    block = min(512, length)
    scale = 1.0 / math.sqrt(width)

    def one_block(index):
        start = index * block
        q_blk = lax.dynamic_slice_in_dim(query, start, block, 0)
        scores = masked_scores(q_blk, keys, start, scale)
        log_total = jnp.log(jnp.sum(jnp.exp(scores), axis=-1))
        probs = jnp.exp(scores - log_total[:, :, None]).astype(jnp.bfloat16)
        attended = jnp.einsum("gqk,kgd->qgd", probs, values, preferred_element_type=jnp.float32)
        return (attended.astype(jnp.bfloat16), log_total)

    outs, logs = lax.map(one_block, jnp.arange(length // block, dtype=jnp.int32))
    return (outs.reshape(length, groups, width), logs)


def attend_backward(query, keys, values, attended, logs, d_att):
    length, groups, width = query.shape
    block = min(512, length)
    scale = 1.0 / math.sqrt(width)

    def one_block(carry, index):
        d_keys, d_values = carry
        start = index * block
        q_blk = lax.dynamic_slice_in_dim(query, start, block, 0)
        o_blk = lax.dynamic_slice_in_dim(attended, start, block, 0)
        do_blk = lax.dynamic_slice_in_dim(d_att, start, block, 0)
        scores = masked_scores(q_blk, keys, start, scale)
        log_total = lax.dynamic_index_in_dim(logs, index, 0, keepdims=False)
        probs = jnp.exp(scores - log_total[:, :, None])
        probs_b = probs.astype(jnp.bfloat16)
        d_values = d_values + jnp.einsum(
            "gqk,qgd->kgd", probs_b, do_blk, preferred_element_type=jnp.float32
        )
        d_probs = jnp.einsum("qgd,kgd->gqk", do_blk, values, preferred_element_type=jnp.float32)
        delta = jnp.swapaxes(
            jnp.sum(do_blk.astype(jnp.float32) * o_blk.astype(jnp.float32), axis=-1), 0, 1
        )
        d_scores = (probs * (d_probs - delta[:, :, None]) * scale).astype(jnp.bfloat16)
        d_query = jnp.einsum(
            "gqk,kgd->qgd", d_scores, keys, preferred_element_type=jnp.float32
        ).astype(jnp.bfloat16)
        d_keys = d_keys + jnp.einsum(
            "gqk,qgd->kgd", d_scores, q_blk, preferred_element_type=jnp.float32
        )
        return ((d_keys, d_values), d_query)

    zeros = jnp.zeros((length, groups, width), jnp.float32)
    (d_keys, d_values), d_queries = lax.scan(
        one_block, (zeros, zeros), jnp.arange(length // block, dtype=jnp.int32)
    )
    return (
        d_queries.reshape(length, groups, width),
        d_keys.astype(jnp.bfloat16),
        d_values.astype(jnp.bfloat16),
    )


def col_dot(left, right):
    return lax.dot_general(
        left, right, (((0,), (0,)), ((), ())), preferred_element_type=jnp.float32
    )


def row_dot(left, right):
    return lax.dot_general(
        left, right, (((1,), (1,)), ((), ())), preferred_element_type=jnp.float32
    )


def per_device(
    tokens,
    ln1_gain,
    ln1_bias,
    w_qkv,
    bias_query,
    bias_value,
    w_out,
    bias_out,
    ln2_gain,
    ln2_bias,
    w_in,
    bias_in,
    w_back,
    bias_back,
    cotangent,
):
    f32 = jnp.float32
    params = (
        lax.all_gather(ln1_gain, ("seq", "shard"), axis=0, tiled=True),
        lax.all_gather(ln1_bias, ("seq", "shard"), axis=0, tiled=True),
        lax.all_gather(w_qkv, ("seq", "shard"), axis=0, tiled=True),
        lax.all_gather(bias_query, ("seq", "shard"), axis=0, tiled=True),
        lax.all_gather(bias_value, ("seq", "shard"), axis=0, tiled=True),
        lax.all_gather(w_out, ("seq", "shard"), axis=0, tiled=True),
        lax.all_gather(bias_out, ("seq", "shard"), axis=0, tiled=True),
        lax.all_gather(ln2_gain, ("seq", "shard"), axis=0, tiled=True),
        lax.all_gather(ln2_bias, ("seq", "shard"), axis=0, tiled=True),
        lax.all_gather(w_in, ("seq", "shard"), axis=0, tiled=True),
        lax.all_gather(bias_in, ("seq", "shard"), axis=0, tiled=True),
        lax.all_gather(w_back, ("seq", "shard"), axis=0, tiled=True),
        lax.all_gather(bias_back, ("seq", "shard"), axis=0, tiled=True),
    )
    (
        g_one,
        s_one,
        full_qkv,
        full_bq,
        full_bv,
        full_out,
        full_bo,
        g_two,
        s_two,
        full_in,
        full_bin,
        full_back,
        full_bback,
    ) = params
    rows = tokens.shape[1]
    width = tokens.shape[2]
    x_f = tokens[0].astype(f32)
    normed1, scale1 = normalize(x_f)
    h_one = (normed1 * g_one.astype(f32) + s_one.astype(f32)).astype(jnp.bfloat16)
    bias_qkv = jnp.concatenate([full_bq.astype(f32), jnp.zeros((width,), f32), full_bv.astype(f32)])
    qkv = (jnp.dot(h_one, full_qkv, preferred_element_type=f32) + bias_qkv).astype(jnp.bfloat16)
    grouped = lax.all_to_all(
        qkv.reshape(rows, 3, width), "seq", split_axis=2, concat_axis=0, tiled=True
    )
    length = grouped.shape[0]
    local_width = grouped.shape[2]
    groups = local_width // HEAD_DIM
    query = grouped[:, 0].reshape(length, groups, HEAD_DIM)
    keys = grouped[:, 1].reshape(length, groups, HEAD_DIM)
    values = grouped[:, 2].reshape(length, groups, HEAD_DIM)
    attended, logs = attend_forward(query, keys, values)
    att_tok = lax.all_to_all(
        attended.reshape(length, local_width), "seq", split_axis=0, concat_axis=1, tiled=True
    )
    resid = x_f + jnp.dot(att_tok, full_out, preferred_element_type=f32) + full_bo.astype(f32)
    normed2, scale2 = normalize(resid)
    h_two = (normed2 * g_two.astype(f32) + s_two.astype(f32)).astype(jnp.bfloat16)
    pre = jnp.dot(h_two, full_in, preferred_element_type=f32) + full_bin.astype(f32)
    act_val, slope = gelu_pair(pre)
    act = act_val.astype(jnp.bfloat16)
    result = (
        resid + jnp.dot(act, full_back, preferred_element_type=f32) + full_bback.astype(f32)
    ).astype(jnp.bfloat16)
    cot_b = cotangent[0]
    cot_f = cot_b.astype(f32)
    g_w_back = col_dot(act, cot_b)
    g_b_back = jnp.sum(cot_f, axis=0)
    d_pre = (row_dot(cot_b, full_back) * slope).astype(jnp.bfloat16)
    g_w_in = col_dot(h_two, d_pre)
    g_b_in = jnp.sum(d_pre.astype(f32), axis=0)
    d_h2 = row_dot(d_pre, full_in)
    g_g2 = jnp.sum(d_h2 * normed2, axis=0)
    g_s2 = jnp.sum(d_h2, axis=0)
    d_resid = cot_f + norm_back(d_h2 * g_two.astype(f32), normed2, scale2)
    d_resid_b = d_resid.astype(jnp.bfloat16)
    g_w_out = col_dot(att_tok, d_resid_b)
    g_b_out = jnp.sum(d_resid, axis=0)
    d_att_tok = row_dot(d_resid_b, full_out).astype(jnp.bfloat16)
    d_att = lax.all_to_all(d_att_tok, "seq", split_axis=1, concat_axis=0, tiled=True).reshape(
        length, groups, HEAD_DIM
    )
    d_query, d_keys, d_values = attend_backward(query, keys, values, attended, logs, d_att)
    stacked = jnp.stack(
        [
            d_query.reshape(length, local_width),
            d_keys.reshape(length, local_width),
            d_values.reshape(length, local_width),
        ],
        axis=1,
    )
    d_qkv = lax.all_to_all(stacked, "seq", split_axis=0, concat_axis=2, tiled=True).reshape(
        rows, 3 * width
    )
    g_w_qkv = col_dot(h_one, d_qkv)
    g_bq = jnp.sum(d_qkv[:, :width].astype(f32), axis=0)
    g_bv = jnp.sum(d_qkv[:, 2 * width :].astype(f32), axis=0)
    d_h1 = row_dot(d_qkv, full_qkv)
    g_g1 = jnp.sum(d_h1 * normed1, axis=0)
    g_s1 = jnp.sum(d_h1, axis=0)
    d_tokens = d_resid + norm_back(d_h1 * g_one.astype(f32), normed1, scale1)
    summed = (
        lax.psum_scatter(g_g1, ("seq", "shard"), scatter_dimension=0, tiled=True),
        lax.psum_scatter(g_s1, ("seq", "shard"), scatter_dimension=0, tiled=True),
        lax.psum_scatter(g_w_qkv, ("seq", "shard"), scatter_dimension=0, tiled=True),
        lax.psum_scatter(g_bq, ("seq", "shard"), scatter_dimension=0, tiled=True),
        lax.psum_scatter(g_bv, ("seq", "shard"), scatter_dimension=0, tiled=True),
        lax.psum_scatter(g_w_out, ("seq", "shard"), scatter_dimension=0, tiled=True),
        lax.psum_scatter(g_b_out, ("seq", "shard"), scatter_dimension=0, tiled=True),
        lax.psum_scatter(g_g2, ("seq", "shard"), scatter_dimension=0, tiled=True),
        lax.psum_scatter(g_s2, ("seq", "shard"), scatter_dimension=0, tiled=True),
        lax.psum_scatter(g_w_in, ("seq", "shard"), scatter_dimension=0, tiled=True),
        lax.psum_scatter(g_b_in, ("seq", "shard"), scatter_dimension=0, tiled=True),
        lax.psum_scatter(g_w_back, ("seq", "shard"), scatter_dimension=0, tiled=True),
        lax.psum_scatter(g_b_back, ("seq", "shard"), scatter_dimension=0, tiled=True),
    )
    (
        r_g1,
        r_s1,
        r_w_qkv,
        r_bq,
        r_bv,
        r_w_out,
        r_b_out,
        r_g2,
        r_s2,
        r_w_in,
        r_b_in,
        r_w_back,
        r_b_back,
    ) = summed
    return (
        result[None],
        d_tokens[None],
        r_g1,
        r_s1,
        r_w_qkv,
        r_bq,
        r_bv,
        r_w_out,
        r_b_out,
        r_g2,
        r_s2,
        r_w_in,
        r_b_in,
        r_w_back,
        r_b_back,
    )


def solution(mesh):
    return jax.shard_map(
        per_device,
        mesh=mesh,
        in_specs=(
            P("shard", "seq", None),
            P(("seq", "shard")),
            P(("seq", "shard")),
            P(("seq", "shard"), None),
            P(("seq", "shard")),
            P(("seq", "shard")),
            P(("seq", "shard"), None),
            P(("seq", "shard")),
            P(("seq", "shard")),
            P(("seq", "shard")),
            P(("seq", "shard"), None),
            P(("seq", "shard")),
            P(("seq", "shard"), None),
            P(("seq", "shard")),
            P("shard", "seq", None),
        ),
        out_specs=(
            P("shard", "seq", None),
            P("shard", "seq", None),
            P(("seq", "shard")),
            P(("seq", "shard")),
            P(("seq", "shard"), None),
            P(("seq", "shard")),
            P(("seq", "shard")),
            P(("seq", "shard"), None),
            P(("seq", "shard")),
            P(("seq", "shard")),
            P(("seq", "shard")),
            P(("seq", "shard"), None),
            P(("seq", "shard")),
            P(("seq", "shard"), None),
            P(("seq", "shard")),
        ),
        check_vma=False,
    )
```

profile of v0, /device:TPU:13, one launch (start us, length us, event | category | flops | bytes accessed | tf_op | source)
XLA Modules:
  0.0 1236.6 jit_solution(11690931587588916261)
XLA Ops:
  16.1 40.8 %all-reduce.18 = (bf16[1024]{0:T(1024)(128)(2,1)S(1)}, bf16[1024]{0:T(1024)(128)(2,1)S(1)}, bf16[1024]{0:T(1024)(128)(2,1)S(1)}, bf16[1024]{0:T(1024)(128)(2,1)S...) all-reduce(bf16[1024]{0:T(1024)(128)(2,1)S(1)} %dynamic-update-slic, ...), channel_id=1, replica_groups=mesh['seq'=4,'shard'=8] {'seq','shard'}, use_global_device_ids=true, to_apply=%add.3 | all-reduce | flops 8192 | bytes 32768
  60.1 21.6 %all-gather.6.cloned.1.call-done = bf16[1024,3072]{1,0:T(8,128)(2,1)} async-done(((bf16[32,3072]{1,0:T(8,128)(2,1)}), bf16[1024,3072]{1,0:T(8,128)(2,1)}) %all-gather.6.cloned.1.call-update) | async-done | bytes 6291472 | tf_op jit(solution)/shard_map/all_gather | solution.py:143
  81.7 8.4 add_convert_fusion
  103.5 101.0 %all-to-all-done = bf16[512,3,1024]{0,1,2:T(4,128)(2,1)} async-done(((bf16[512,3,1024]{0,1,2:T(4,128)(2,1)}), bf16[512,3,1024]{0,1,2:T(4,128)(2,1)}, u32[]{:S(2)}, u32[]{:S(2)}) %all-to-all-start) | async-done | bytes 3145760 | tf_op jit(solution)/shard_map/all_to_all | solution.py:177
  216.3 50.8 %while.27 = (s32[]{:T(128)}, bf16[4,512,4,64]{1,3,2,0:T(8,128)(2,1)}, f32[4,4,512]{2,1,0:T(4,128)}, s32[4]{0:T(128)S(1)}, bf16[2048,4,64]{0,2,1:T(8,128)(2,1)S(1...) while((s32[]{:T(128)}, ...), condition=%wide.region_4.5_spmd, body=%wide.region_2.4_spmd.sunk | while | flops 1104280064 | bytes 43569372 | solution.py:64
  268.1 7.5 all-to-all-start.1
  275.6 54.4 %all-gather = bf16[32,1,128]{2,1,0:T(2,128)(2,1)S(1)} all-gather(bf16[1,1,128]{2,1,0:T(2,128)(2,1)S(1)} %bitcast.188), channel_id=1, replica_groups=mesh['seq'=4,'shard'=8] {'seq','shard'}, dimensions={0}, use_global_device_ids=true | all-gather | bytes 8448 | tf_op jit(solution)/shard_map/all_gather | solution.py:151
  335.1 10.6 fusion.83
  345.7 11.9 all-gather.12.cloned.1.call-done
  357.6 14.9 %convert_reduce_fusion = (f32[4096]{0:T(1024)}, bf16[512,4096]{1,0:T(8,128)(2,1)}) fusion(f32[512,4096]{1,0:T(8,128)} %fusion.83, f32[4096]{0:T(1024)S(1)} %bitcast.185, bf16[4096,1024]{1,0:T(8,128)(2,1)} %all-gather.12.cloned.1.call-done, bf16[1,512,1024]{2,1,0:T(8,128)(2,1)} %param.33), kind=kOutput, calls=%fused_computation.52 | convolution fusion | flops 4341100544 | bytes 22052864 | tf_op jit(solution)/shard_map/dot_general | solution.py:117
  372.5 7.7 multiply_reduce_fusion.1
  397.3 15.6 %all-to-all-done.2 = bf16[512,4,256]{2,0,1:T(8,128)(2,1)} async-done(((bf16[512,4,256]{2,0,1:T(8,128)(2,1)}), bf16[512,4,256]{2,0,1:T(8,128)(2,1)}, u32[]{:S(2)}, u32[]{:S(2)}) %all-to-all-start.2) | async-done | bytes 1048608 | tf_op jit(solution)/shard_map/all_to_all | solution.py:214
  416.7 156.1 %while.28 = (s32[]{:T(128)}, f32[2048,4,64]{0,2,1:T(8,128)}, f32[2048,4,64]{0,2,1:T(8,128)}, bf16[4,512,4,64]{1,3,2,0:T(8,128)(2,1)}, s32[4]{0:T(128)S(1)}, /*in...) while((s32[]{:T(128)}, f32[2048,4,64]{0,2,1:T(8,128)}, ...), condition=%wide.region_11.12_spmd.clone, body=%wide.region_9.11_spmd.clone.sunk | while | flops 2734291456 | bytes 138236336 | solution.py:100
  426.2 7.2 fusion.140
  433.4 10.5 multiply_convert_fusion.5
  443.9 7.0 fusion.141
  464.3 7.6 fusion.140
  471.9 10.5 multiply_convert_fusion.5
  503.4 7.6 fusion.140
  511.0 10.5 multiply_convert_fusion.5
  542.5 7.6 fusion.140
  550.1 10.5 multiply_convert_fusion.5
  583.7 97.2 %all_to_all.68 = bf16[2048,3,256]{2,1,0:T(4,128)(2,1)S(1)} all-to-all(bf16[2048,3,256]{2,1,0:T(4,128)(2,1)} %copy.82), channel_id=1, replica_groups=mesh['seq'=4,'shard'=8] {'seq'}, dimensions={0} | all-to-all | bytes 6291456 | tf_op jit(solution)/shard_map/all_to_all | solution.py:226
  687.8 8.7 fusion.65
  697.7 16.2 %fusion.68 = f32[4096,1024]{1,0:T(8,128)} fusion(bf16[1,512,1024]{2,1,0:T(8,128)(2,1)S(1)} %copy-done.16, f32[512,4096]{1,0:T(8,128)} %fusion.83, f32[4096]{0:T(1024)S(1)} %bitcast.186), kind=kOutput, calls=%fused_computation.98 | convolution fusion | flops 4315938816 | bytes 26230784 | tf_op jit(solution)/shard_map/dot_general | solution.py:111
  715.7 11.5 fusion.82
  727.8 13.2 %fusion.63 = bf16[1,512,1024]{2,1,0:T(8,128)(2,1)} fusion(f32[512,1024]{1,0:T(8,128)S(1)} %copy-done.6, bf16[4096,1024]{1,0:T(8,128)(2,1)} %all-gather.12.cloned.1.call-done, f32[1024]{0:T(1024)S(1)} %convert_element_type.124, f32[512,4096]{1,0:T(8,128)} %fusion.83, f32[4096]{0:T(1024)S(1)} %bitcast.187), kind=kOutput, calls=%fused_computation.94 | convolution fusion | flops 4317511680 | bytes 19943424 | tf_op jit(solution)/shard_map/dot_general | solution.py:197
  741.5 8.8 fusion.56
  750.3 45.6 %all-reduce.17 = (f32[1024]{0:T(1024)S(1)}, f32[1024]{0:T(1024)S(1)}, f32[1024]{0:T(1024)S(1)}, f32[1024]{0:T(1024)S(1)}, f32[1024]{0:T(1024)S(1)}, /*index=5*/f...) all-reduce(f32[1024]{0:T(1024)S(1)} %get-tuple-element.184, ...), channel_id=2, replica_groups=mesh['seq'=4,'shard'=8] {'seq','shard'}, use_global_device_ids=true, to_apply=%region_15.16.clone | all-reduce | flops 12288 | bytes 98304
  804.8 48.2 %reduce-scatter.5.cloned.1.call-done = f32[32,3072]{1,0:T(8,128)} async-done(((f32[1024,3072]{1,0:T(8,128)}), f32[32,3072]{1,0:T(8,128)}) %reduce-scatter.5.cloned.1.call-update) | async-done | bytes 393232 | tf_op jit(solution)/shard_map/reduce_scatter | solution.py:239
  853.0 189.0 %reduce-scatter.11.cloned.1.call-done = f32[128,1024]{1,0:T(8,128)} async-done(((f32[4096,1024]{1,0:T(8,128)}), f32[128,1024]{1,0:T(8,128)}) %reduce-scatter.11.cloned.1.call-update) | async-done | bytes 524304 | tf_op jit(solution)/shard_map/reduce_scatter | solution.py:248
  1042.1 187.5 %reduce-scatter.9.cloned.1.call-done = f32[32,4096]{1,0:T(8,128)} async-done(((f32[1024,4096]{1,0:T(8,128)}), f32[32,4096]{1,0:T(8,128)}) %reduce-scatter.9.cloned.1.call-update) | async-done | bytes 524304 | tf_op jit(solution)/shard_map/reduce_scatter | solution.py:246
  (286 shorter events, 208.4 us)
Async XLA Ops:
  7.2 74.5 %all-gather.6.cloned.1.call-start = ((), (), s32[]{:S(2)}) async-start(), calls=%async_computation.8 | async-start | bytes 6488064 | tf_op jit(solution)/shard_map/all_gather | solution.py:143
  7.9 322.1 %all-gather.8.cloned.1.call-start = ((), (), s32[]{:S(2)}) async-start(), calls=%async_computation.9 | async-start | bytes 2162688 | tf_op jit(solution)/shard_map/all_gather | solution.py:146
  8.7 326.5 %all-gather.10.cloned.1.call-start = ((), (), s32[]{:S(2)}) async-start(), calls=%async_computation.10 | async-start | bytes 8650752 | tf_op jit(solution)/shard_map/all_gather | solution.py:150
  56.9 24.8 %copy-start.25 = (f32[1024]{0:T(1024)}, f32[1024]{0:T(1024)S(1)}, u32[]{:S(2)}) copy-start(f32[1024]{0:T(1024)S(1)} %convert_element_type.112) | copy-start | bytes 12292
  56.9 24.8 %copy-start.38 = (f32[1024]{0:T(1024)}, f32[1024]{0:T(1024)S(1)}, u32[]{:S(2)}) copy-start(f32[1024]{0:T(1024)S(1)} %convert_element_type.113) | copy-start | bytes 12292
  58.4 23.3 %copy-start.21 = (f32[512]{0:T(512)}, f32[512]{0:T(512)S(1)}, u32[]{:S(2)}) copy-start(f32[512]{0:T(512)S(1)} %broadcast_multiply_fusion.5) | copy-start | bytes 6148
  60.1 21.7 %copy-start.34 = (f32[512]{0:T(512)}, f32[512]{0:T(512)S(1)}, u32[]{:S(2)}) copy-start(f32[512]{0:T(512)S(1)} %add_rsqrt_fusion.1) | copy-start | bytes 6148
  97.9 106.6 %all-to-all-start = ((bf16[512,3,1024]{0,1,2:T(4,128)(2,1)}), bf16[512,3,1024]{0,1,2:T(4,128)(2,1)}, u32[]{:S(2)}, u32[]{:S(2)}) async-start(bf16[512,3,1024]{0,1,2:T(4,128)(2,1)} %copy.72), calls=%async_computation | async-start | bytes 8388608 | tf_op jit(solution)/shard_map/all_to_all | solution.py:177
  103.0 254.6 %all-gather.12.cloned.1.call-start = ((), (), s32[]{:S(2)}) async-start(), calls=%async_computation.11 | async-start | bytes 8650752 | tf_op jit(solution)/shard_map/all_gather | solution.py:152
  216.3 59.3 %copy-start.43 = (bf16[128]{0:T(256)(128)(2,1)S(1)}, bf16[128]{0:T(256)(128)(2,1)}, u32[]{:S(2)}) copy-start(bf16[128]{0:T(256)(128)(2,1)} %param.30) | copy-start | bytes 772
  268.1 61.9 %all-to-all-start.1 = ((bf16[4,512,256]{1,2,0:T(8,128)(2,1)}), bf16[4,512,256]{1,2,0:T(8,128)(2,1)S(1)}, u32[]{:S(2)}, u32[]{:S(2)}) async-start(bf16[4,512,256]{1,2,0:T(8,128)(2,1)} %bitcast.12), calls=%async_computation.1 | async-start | bytes 2097152 | tf_op jit(solution)/shard_map/all_to_all | solution.py:187
  275.6 104.6 %copy-start.27 = (f32[1024]{0:T(1024)}, f32[1024]{0:T(1024)S(1)}, u32[]{:S(2)}) copy-start(f32[1024]{0:T(1024)S(1)} %convert_element_type.119) | copy-start | bytes 12292
  275.6 59.6 %copy-start.40 = (f32[1024]{0:T(1024)}, f32[1024]{0:T(1024)S(1)}, u32[]{:S(2)}) copy-start(f32[1024]{0:T(1024)S(1)} %convert_element_type.120) | copy-start | bytes 12292
  330.0 27.6 %copy-start.30 = (f32[32,1,128]{2,1,0:T(1,128)}, f32[32,1,128]{2,1,0:T(1,128)S(1)}, u32[]{:S(2)}) copy-start(f32[32,1,128]{2,1,0:T(1,128)S(1)} %convert_element_type.137) | copy-start | bytes 49156
  334.7 37.8 %copy-start.5 = (f32[512,1024]{1,0:T(8,128)}, f32[512,1024]{1,0:T(8,128)S(1)}, u32[]{:S(2)}) copy-start(f32[512,1024]{1,0:T(8,128)S(1)} %get-tuple-element.254) | copy-start | bytes 6291460
  334.7 45.5 %copy-start.19 = (f32[512]{0:T(512)}, f32[512]{0:T(512)S(1)}, u32[]{:S(2)}) copy-start(f32[512]{0:T(512)S(1)} %broadcast_multiply_fusion.4) | copy-start | bytes 6148
  335.1 45.1 %copy-start.32 = (f32[512]{0:T(512)}, f32[512]{0:T(512)S(1)}, u32[]{:S(2)}) copy-start(f32[512]{0:T(512)S(1)} %add_rsqrt_fusion) | copy-start | bytes 6148
  357.6 14.9 %copy-start.44 = (bf16[1024,4096]{1,0:T(8,128)(2,1)S(1)}, bf16[1024,4096]{1,0:T(8,128)(2,1)}, u32[]{:S(2)}) copy-start(bf16[1024,4096]{1,0:T(8,128)(2,1)} %all-gather.10.cloned.1.call-done) | copy-start | bytes 25165828
  372.5 7.7 copy-start.15
  383.6 9.2 copy-start.3
  385.9 27.0 %all-to-all-start.2 = ((bf16[512,4,256]{2,0,1:T(8,128)(2,1)}), bf16[512,4,256]{2,0,1:T(8,128)(2,1)}, u32[]{:S(2)}, u32[]{:S(2)}) async-start(bf16[512,4,256]{2,0,1:T(8,128)(2,1)} %bitcast.179), calls=%async_computation.2 | async-start | bytes 2097152 | tf_op jit(solution)/shard_map/all_to_all | solution.py:214
  390.4 414.4 %reduce-scatter.7.cloned.1.call-start = ((), (), s32[]{:S(2)}) async-start(), calls=%async_computation.13 | async-start | bytes 4325376 | tf_op jit(solution)/shard_map/reduce_scatter | solution.py:242
  397.2 455.8 %reduce-scatter.5.cloned.1.call-start = ((), (), s32[]{:S(2)}) async-start(), calls=%async_computation.12 | async-start | bytes 12976128 | tf_op jit(solution)/shard_map/reduce_scatter | solution.py:239
  696.5 345.6 %reduce-scatter.11.cloned.1.call-start = ((), (), s32[]{:S(2)}) async-start(), calls=%async_computation.15 | async-start | bytes 17301504 | tf_op jit(solution)/shard_map/reduce_scatter | solution.py:248
  714.0 515.6 %reduce-scatter.9.cloned.1.call-start = ((), (), s32[]{:S(2)}) async-start(), calls=%async_computation.14 | async-start | bytes 17301504 | tf_op jit(solution)/shard_map/reduce_scatter | solution.py:246
  727.8 13.2 %copy-start.10 = (bf16[512,3,4,256]{0,3,2,1:T(8,128)(2,1)S(1)}, bf16[512,3,4,256]{0,3,2,1:T(8,128)(2,1)}, u32[]{:S(2)}) copy-start(bf16[512,3,4,256]{0,3,2,1:T(8,128)(2,1)} %copy.84) | copy-start | bytes 9437188
  741.4 8.8 copy-start.23
  741.4 8.8 copy-start.24
  741.4 8.8 copy-start.29
  741.4 8.8 copy-start.36
  741.4 8.8 copy-start.37
  741.5 59.7 %copy-start.4 = (f32[512,1024]{1,0:T(8,128)S(1)}, f32[512,1024]{1,0:T(8,128)}, u32[]{:S(2)}) copy-start(f32[512,1024]{1,0:T(8,128)} %copy-done.3) | copy-start | bytes 6291460
  (42 other events, 167.6 us)
Sparse Core Ops, SparseCore 0:
  10.8 70.8 all-gather.5
  84.6 102.7 all-gather.7
  190.2 78.1 all-gather.9
  271.1 86.4 all-gather.11
  397.4 115.2 reduce-scatter.6
  696.6 156.3 reduce-scatter.4
  855.9 186.1 reduce-scatter.10
  1044.9 184.6 reduce-scatter.8
where the time goes:
time: 1250 us; the launch traced here: 1240 us
  waiting for transfers between devices  577 us (46%)
  matrix products  282 us (23%)
  blocking collectives  238 us (19%)
  local copies, waits for them, and re-layouts  70.1 us (6%)
  other arithmetic  22.6 us (2%)
  starting transfers between devices  17.6 us (1%)
  between operations  14.8 us (1%)
  loops' own time  14 us (1%)
    reduce_scatter x1, waiting for transfers between devices, per_device(): lax.psum_scatter(g_w_back, ('seq', 'shard'), scatter_dimension=0, tiled=T...  189 us
    reduce_scatter x1, waiting for transfers between devices, per_device(): lax.psum_scatter(g_w_in, ('seq', 'shard'), scatter_dimension=0, tiled=True)  188 us
    all_to_all x1, waiting for transfers between devices, per_device(): lax.all_to_all(qkv.reshape(rows, 3, width), 'seq', split_axis=2, concat_a...  101 us
    all_to_all x1, blocking collectives, per_device(): lax.all_to_all(stacked, 'seq', split_axis=0, concat_axis=2, tiled=True)  97.2 us
    unnamed x2, blocking collectives  86.4 us
    all_gather x1, blocking collectives, per_device(): lax.all_gather(bias_in, ('seq', 'shard'), axis=0, tiled=True)  54.4 us
    reduce_scatter x1, waiting for transfers between devices, per_device(): lax.psum_scatter(g_w_qkv, ('seq', 'shard'), scatter_dimension=0, tiled=True)  48.2 us
    dot_general x4, matrix products, one_block(): jnp.einsum('qgd,kgd->gqk', do_blk, values, preferred_element_type=jnp.flo...  42 us
  transfers between devices with their start and end apart: 11, of which 7 were waited for; matrix products, arithmetic and copies ran while one was open for 28% of the time, Pallas kernels for 0%

commit v1 on v0

--- a/solution.py
+++ b/solution.py
@@ -7,6 +7,18 @@
 HEAD_DIM = 64
 norm_eps = 1e-05
 gelu_c = math.sqrt(2.0 / math.pi)
+
+
+def cut_along(x, dim, count):
+    lengths = x.shape
+    blocks = x.reshape(*lengths[:dim], count, lengths[dim] // count, *lengths[dim + 1 :])
+    return jnp.moveaxis(blocks, dim, 0)
+
+
+def joined_along(pieces, dim):
+    dims = list(pieces.shape[1:])
+    dims[dim] *= pieces.shape[0]
+    return jnp.moveaxis(pieces, 0, dim).reshape(dims)
 
 
 def normalize(values):
@@ -174,9 +186,15 @@
     h_one = (normed1 * g_one.astype(f32) + s_one.astype(f32)).astype(jnp.bfloat16)
     bias_qkv = jnp.concatenate([full_bq.astype(f32), jnp.zeros((width,), f32), full_bv.astype(f32)])
     qkv = (jnp.dot(h_one, full_qkv, preferred_element_type=f32) + bias_qkv).astype(jnp.bfloat16)
-    grouped = lax.all_to_all(
-        qkv.reshape(rows, 3, width), "seq", split_axis=2, concat_axis=0, tiled=True
-    )
+    shard = qkv.reshape(rows, 3, width)
+    peers, place = (lax.axis_size("seq"), lax.axis_index("seq"))
+    pieces = cut_along(shard, 2, peers)
+    outs_2 = [pieces[place]]
+    for hop in range(1, peers):
+        sent = pieces[place ^ hop]
+        outs_2.append(lax.ppermute(sent, "seq", [(i, i ^ hop) for i in range(peers)]))
+    pieces = jnp.stack(outs_2)[place ^ jnp.arange(peers)]
+    grouped = joined_along(pieces, 0)
     length = grouped.shape[0]
     local_width = grouped.shape[2]
     groups = local_width // HEAD_DIM

time: 1250 us -> 1230 us (0.984)
  waiting for transfers between devices: 577 us -> 552 us
    all_to_all x1 -> x0, waiting for transfers between devices: 101 us -> none  [per_device(): lax.all_to_all(qkv.reshape(rows, 3, width), 'seq', split_axis=2, concat_a...]
    ppermute x0 -> x3, waiting for transfers between devices: none -> 74 us  [per_device(): lax.ppermute(sent, 'seq', [(i, i ^ hop) for i in range(peers)])]
    another operation x2 -> x4, local copies, waits for them, and re-layouts: 2.15 us -> 15 us
  transfers between devices with their start and end apart: 11 -> 13, of which waited for: 7 -> 9; matrix products, arithmetic and copies ran while one was open for 28% -> 29% of each run, Pallas kernels for 0% -> 0%
where the time goes in v1:
time: 1230 us; the launch traced here: 1220 us
  waiting for transfers between devices  552 us (45%)
  matrix products  283 us (23%)
  blocking collectives  238 us (19%)
  local copies, waits for them, and re-layouts  75.2 us (6%)
  other arithmetic  24.5 us (2%)
  between operations  14.9 us (1%)
  loops' own time  14.5 us (1%)
  starting transfers between devices  13.4 us (1%)
    reduce_scatter x1, waiting for transfers between devices, per_device(): lax.psum_scatter(g_w_back, ('seq', 'shard'), scatter_dimension=0, tiled=T...  189 us
    reduce_scatter x1, waiting for transfers between devices, per_device(): lax.psum_scatter(g_w_in, ('seq', 'shard'), scatter_dimension=0, tiled=True)  188 us
    all_to_all x1, blocking collectives, per_device(): lax.all_to_all(stacked, 'seq', split_axis=0, concat_axis=2, tiled=True)  97.2 us
    unnamed x2, blocking collectives  86.3 us
    ppermute x3, waiting for transfers between devices, per_device(): lax.ppermute(sent, 'seq', [(i, i ^ hop) for i in range(peers)])  74 us
    all_gather x1, blocking collectives, per_device(): lax.all_gather(bias_in, ('seq', 'shard'), axis=0, tiled=True)  55 us
    reduce_scatter x1, waiting for transfers between devices, per_device(): lax.psum_scatter(g_w_qkv, ('seq', 'shard'), scatter_dimension=0, tiled=True)  48.3 us
    dot_general x4, matrix products, one_block(): jnp.einsum('qgd,kgd->gqk', do_blk, values, preferred_element_type=jnp.flo...  42.3 us
  transfers between devices with their start and end apart: 13, of which 9 were waited for; matrix products, arithmetic and copies ran while one was open for 29% of the time, Pallas kernels for 0%

profile of v1, /device:TPU:13, one launch (start us, length us, event | category | flops | bytes accessed | tf_op | source)
XLA Modules:
  0.0 1215.3 jit_solution(4173483604680152435)
XLA Ops:
  16.2 40.6 %all-reduce.18 = (bf16[1024]{0:T(1024)(128)(2,1)S(1)}, bf16[1024]{0:T(1024)(128)(2,1)S(1)}, bf16[1024]{0:T(1024)(128)(2,1)S(1)}, bf16[1024]{0:T(1024)(128)(2,1)S...) all-reduce(bf16[1024]{0:T(1024)(128)(2,1)S(1)} %dynamic-update-slic, ...), channel_id=1, replica_groups=mesh['seq'=4,'shard'=8] {'seq','shard'}, use_global_device_ids=true, to_apply=%add.3 | all-reduce | flops 8192 | bytes 32768
  60.0 21.7 %all-gather.6.cloned.1.call-done = bf16[1024,3072]{1,0:T(8,128)(2,1)} async-done(((bf16[32,3072]{1,0:T(8,128)(2,1)}), bf16[1024,3072]{1,0:T(8,128)(2,1)}) %all-gather.6.cloned.1.call-update) | async-done | bytes 6291472 | tf_op jit(solution)/shard_map/all_gather | solution.py:155
  81.7 8.4 add_convert_fusion
  95.6 7.3 constant_dynamic-slice_fusion.3
  108.9 38.0 %collective-permute-done.2 = bf16[512,3,256]{2,0,1:T(8,128)(2,1)S(1)} collective-permute-done((bf16[512,3,256]{2,0,1:T(8,128)(2,1)}, bf16[512,3,256]{2,0,1:T(8,128)(2,1)S(1)}, u32[]{:S(2)}, u32[]{:S(2)}) %collective-permute-start.2) | collective-permute-done | bytes 786464 | tf_op jit(solution)/shard_map/ppermute | solution.py:195
  148.7 34.2 %collective-permute-done.1 = bf16[512,3,256]{2,0,1:T(8,128)(2,1)} collective-permute-done((bf16[512,3,256]{2,0,1:T(8,128)(2,1)}, bf16[512,3,256]{2,0,1:T(8,128)(2,1)}, u32[]{:S(2)}, u32[]{:S(2)}) %collective-permute-start.1) | collective-permute-done | bytes 786464 | tf_op jit(solution)/shard_map/ppermute | solution.py:195
  193.4 51.3 %while.27 = (s32[]{:T(128)}, bf16[4,512,4,64]{1,3,2,0:T(8,128)(2,1)}, f32[4,4,512]{2,1,0:T(4,128)}, s32[4]{0:T(128)S(1)}, bf16[2048,4,64]{0,2,1:T(8,128)(2,1)S(1...) while((s32[]{:T(128)}, ...), condition=%wide.region_4.5_spmd, body=%wide.region_2.4_spmd.sunk | while | flops 1104280064 | bytes 43569372 | solution.py:76
  251.7 55.0 %all-gather = bf16[32,1,128]{2,1,0:T(2,128)(2,1)S(1)} all-gather(bf16[1,1,128]{2,1,0:T(2,128)(2,1)S(1)} %bitcast.202), channel_id=1, replica_groups=mesh['seq'=4,'shard'=8] {'seq','shard'}, dimensions={0}, use_global_device_ids=true | all-gather | bytes 8448 | tf_op jit(solution)/shard_map/all_gather | solution.py:163
  311.7 10.6 fusion.84
  322.3 13.4 %all-gather.12.cloned.1.call-done = bf16[4096,1024]{1,0:T(8,128)(2,1)} async-done(((bf16[128,1024]{1,0:T(8,128)(2,1)}), bf16[4096,1024]{1,0:T(8,128)(2,1)}) %all-gather.12.cloned.1.call-update) | async-done | bytes 8388624 | tf_op jit(solution)/shard_map/all_gather | solution.py:164
  335.7 15.0 %convert_reduce_fusion = (f32[4096]{0:T(1024)}, bf16[512,4096]{1,0:T(8,128)(2,1)}) fusion(f32[512,4096]{1,0:T(8,128)} %fusion.84, f32[4096]{0:T(1024)S(1)} %bitcast.199, bf16[4096,1024]{1,0:T(8,128)(2,1)} %all-gather.12.cloned.1.call-done, bf16[1,512,1024]{2,1,0:T(8,128)(2,1)} %param.33), kind=kOutput, calls=%fused_computation.53 | convolution fusion | flops 4341100544 | bytes 22052864 | tf_op jit(solution)/shard_map/dot_general | solution.py:129
  350.7 7.7 multiply_reduce_fusion.1
  375.5 15.7 %all-to-all-done.1 = bf16[512,4,256]{2,0,1:T(8,128)(2,1)} async-done(((bf16[512,4,256]{2,0,1:T(8,128)(2,1)}), bf16[512,4,256]{2,0,1:T(8,128)(2,1)}, u32[]{:S(2)}, u32[]{:S(2)}) %all-to-all-start.1) | async-done | bytes 1048608 | tf_op jit(solution)/shard_map/all_to_all | solution.py:232
  395.0 156.4 %while.28 = (s32[]{:T(128)}, f32[2048,4,64]{0,2,1:T(8,128)}, f32[2048,4,64]{0,2,1:T(8,128)}, bf16[4,512,4,64]{1,3,2,0:T(8,128)(2,1)}, s32[4]{0:T(128)S(1)}, /*in...) while((s32[]{:T(128)}, f32[2048,4,64]{0,2,1:T(8,128)}, ...), condition=%wide.region_11.12_spmd.clone, body=%wide.region_9.11_spmd.clone.sunk | while | flops 2734291456 | bytes 138236336 | solution.py:112
  404.5 7.2 fusion.141
  411.7 10.6 multiply_convert_fusion.5
  442.6 7.6 fusion.141
  450.3 10.6 multiply_convert_fusion.5
  481.9 7.6 fusion.141
  489.5 10.6 multiply_convert_fusion.5
  521.0 7.6 fusion.141
  528.7 10.6 multiply_convert_fusion.5
  562.3 97.2 %all_to_all.50 = bf16[2048,3,256]{2,1,0:T(4,128)(2,1)S(1)} all-to-all(bf16[2048,3,256]{2,1,0:T(4,128)(2,1)} %copy.92), channel_id=1, replica_groups=mesh['seq'=4,'shard'=8] {'seq'}, dimensions={0} | all-to-all | bytes 6291456 | tf_op jit(solution)/shard_map/all_to_all | solution.py:244
  666.5 8.6 fusion.65
  676.3 16.2 %fusion.68 = f32[4096,1024]{1,0:T(8,128)} fusion(bf16[1,512,1024]{2,1,0:T(8,128)(2,1)S(1)} %copy-done.17, f32[512,4096]{1,0:T(8,128)} %fusion.84, f32[4096]{0:T(1024)S(1)} %bitcast.200), kind=kOutput, calls=%fused_computation.100 | convolution fusion | flops 4315938816 | bytes 26230784 | tf_op jit(solution)/shard_map/dot_general | solution.py:123
  694.3 11.5 fusion.83
  706.5 13.2 %fusion.63 = bf16[1,512,1024]{2,1,0:T(8,128)(2,1)} fusion(f32[512,1024]{1,0:T(8,128)S(1)} %copy-done.6, bf16[4096,1024]{1,0:T(8,128)(2,1)} %all-gather.12.cloned.1.call-done, f32[1024]{0:T(1024)S(1)} %convert_element_type.124, f32[512,4096]{1,0:T(8,128)} %fusion.84, f32[4096]{0:T(1024)S(1)} %bitcast.201), kind=kOutput, calls=%fused_computation.96 | convolution fusion | flops 4317511680 | bytes 19943424 | tf_op jit(solution)/shard_map/dot_general | solution.py:215
  720.1 8.8 fusion.56
  728.9 45.7 %all-reduce.17 = (f32[1024]{0:T(1024)S(1)}, f32[1024]{0:T(1024)S(1)}, f32[1024]{0:T(1024)S(1)}, f32[1024]{0:T(1024)S(1)}, f32[1024]{0:T(1024)S(1)}, /*index=5*/f...) all-reduce(f32[1024]{0:T(1024)S(1)} %get-tuple-element.184, ...), channel_id=2, replica_groups=mesh['seq'=4,'shard'=8] {'seq','shard'}, use_global_device_ids=true, to_apply=%region_15.16.clone | all-reduce | flops 12288 | bytes 98304
  783.5 48.3 %reduce-scatter.5.cloned.1.call-done = f32[32,3072]{1,0:T(8,128)} async-done(((f32[1024,3072]{1,0:T(8,128)}), f32[32,3072]{1,0:T(8,128)}) %reduce-scatter.5.cloned.1.call-update) | async-done | bytes 393232 | tf_op jit(solution)/shard_map/reduce_scatter | solution.py:257
  831.7 189.0 %reduce-scatter.11.cloned.1.call-done = f32[128,1024]{1,0:T(8,128)} async-done(((f32[4096,1024]{1,0:T(8,128)}), f32[128,1024]{1,0:T(8,128)}) %reduce-scatter.11.cloned.1.call-update) | async-done | bytes 524304 | tf_op jit(solution)/shard_map/reduce_scatter | solution.py:266
  1020.8 187.5 %reduce-scatter.9.cloned.1.call-done = f32[32,4096]{1,0:T(8,128)} async-done(((f32[1024,4096]{1,0:T(8,128)}), f32[32,4096]{1,0:T(8,128)}) %reduce-scatter.9.cloned.1.call-update) | async-done | bytes 524304 | tf_op jit(solution)/shard_map/reduce_scatter | solution.py:264
  (303 shorter events, 219.9 us)
Async XLA Ops:
  7.2 74.5 %all-gather.6.cloned.1.call-start = ((), (), s32[]{:S(2)}) async-start(), calls=%async_computation.7 | async-start | bytes 6488064 | tf_op jit(solution)/shard_map/all_gather | solution.py:155
  7.9 298.8 %all-gather.8.cloned.1.call-start = ((), (), s32[]{:S(2)}) async-start(), calls=%async_computation.8 | async-start | bytes 2162688 | tf_op jit(solution)/shard_map/all_gather | solution.py:158
  8.7 303.1 %all-gather.10.cloned.1.call-start = ((), (), s32[]{:S(2)}) async-start(), calls=%async_computation.9 | async-start | bytes 8650752 | tf_op jit(solution)/shard_map/all_gather | solution.py:162
  9.4 326.3 %all-gather.12.cloned.1.call-start = ((), (), s32[]{:S(2)}) async-start(), calls=%async_computation.10 | async-start | bytes 8650752 | tf_op jit(solution)/shard_map/all_gather | solution.py:164
  56.8 24.9 %copy-start.28 = (f32[1024]{0:T(1024)}, f32[1024]{0:T(1024)S(1)}, u32[]{:S(2)}) copy-start(f32[1024]{0:T(1024)S(1)} %convert_element_type.112) | copy-start | bytes 12292
  56.8 24.9 %copy-start.41 = (f32[1024]{0:T(1024)}, f32[1024]{0:T(1024)S(1)}, u32[]{:S(2)}) copy-start(f32[1024]{0:T(1024)S(1)} %convert_element_type.113) | copy-start | bytes 12292
  58.3 23.4 %copy-start.24 = (f32[512]{0:T(512)}, f32[512]{0:T(512)S(1)}, u32[]{:S(2)}) copy-start(f32[512]{0:T(512)S(1)} %broadcast_multiply_fusion.5) | copy-start | bytes 6148
  60.0 21.7 %copy-start.37 = (f32[512]{0:T(512)}, f32[512]{0:T(512)S(1)}, u32[]{:S(2)}) copy-start(f32[512]{0:T(512)S(1)} %add_rsqrt_fusion.1) | copy-start | bytes 6148
  106.1 40.9 %collective-permute-start.2 = (bf16[512,3,256]{2,0,1:T(8,128)(2,1)}, bf16[512,3,256]{2,0,1:T(8,128)(2,1)S(1)}, u32[]{:S(2)}, u32[]{:S(2)}) collective-permute-start(bf16[512,3,256]{2,0,1:T(8,128)(2,1)} %bitcast.144), channel_id=1, source_target_pairs={{0,24},{8,16},{16,8},{24,0},{1,25},{9,17},{17,9},{25,1},{2,26},{10... | collective-permute-start | bytes 2359304 | tf_op jit(solution)/shard_map/ppermute | solution.py:195
  106.6 42.1 %collective-permute-start = (bf16[512,3,256]{2,0,1:T(8,128)(2,1)}, bf16[512,3,256]{2,0,1:T(8,128)(2,1)S(1)}, u32[]{:S(2)}, u32[]{:S(2)}) collective-permute-start(bf16[512,3,256]{2,0,1:T(8,128)(2,1)} %bitcast.146), channel_id=1, source_target_pairs={{0,8},{8,0},{16,24},{24,16},{1,9},{9,1},{17,25},{25,17},{2,10},{10... | collective-permute-start | bytes 2359304 | tf_op jit(solution)/shard_map/ppermute | solution.py:195
  107.8 75.1 %collective-permute-start.1 = (bf16[512,3,256]{2,0,1:T(8,128)(2,1)}, bf16[512,3,256]{2,0,1:T(8,128)(2,1)}, u32[]{:S(2)}, u32[]{:S(2)}) collective-permute-start(bf16[512,3,256]{2,0,1:T(8,128)(2,1)} %bitcast.145), channel_id=1, source_target_pairs={{0,16},{8,24},{16,0},{24,8},{1,17},{9,25},{17,1},{25,9},{2,18},{10... | collective-permute-start | bytes 2359304 | tf_op jit(solution)/shard_map/ppermute | solution.py:195
  146.9 36.0 %copy-start.19 = (bf16[512,3,256]{2,0,1:T(8,128)(2,1)}, bf16[512,3,256]{2,0,1:T(8,128)(2,1)S(1)}, u32[]{:S(2)}) copy-start(bf16[512,3,256]{2,0,1:T(8,128)(2,1)S(1)} %collective-permute-done.2) | copy-start | bytes 2359300
  148.7 34.2 %copy-start.20 = (bf16[512,3,256]{2,0,1:T(8,128)(2,1)}, bf16[512,3,256]{2,0,1:T(8,128)(2,1)S(1)}, u32[]{:S(2)}) copy-start(bf16[512,3,256]{2,0,1:T(8,128)(2,1)S(1)} %collective-permute-done) | copy-start | bytes 2359300
  193.4 58.3 %copy-start.46 = (bf16[128]{0:T(256)(128)(2,1)S(1)}, bf16[128]{0:T(256)(128)(2,1)}, u32[]{:S(2)}) copy-start(bf16[128]{0:T(256)(128)(2,1)} %param.30) | copy-start | bytes 772
  245.6 61.1 %all-to-all-start = ((bf16[4,512,256]{1,2,0:T(8,128)(2,1)}), bf16[4,512,256]{1,2,0:T(8,128)(2,1)S(1)}, u32[]{:S(2)}, u32[]{:S(2)}) async-start(bf16[4,512,256]{1,2,0:T(8,128)(2,1)} %bitcast.17), calls=%async_computation | async-start | bytes 2097152 | tf_op jit(solution)/shard_map/all_to_all | solution.py:205
  251.7 106.7 %copy-start.30 = (f32[1024]{0:T(1024)}, f32[1024]{0:T(1024)S(1)}, u32[]{:S(2)}) copy-start(f32[1024]{0:T(1024)S(1)} %convert_element_type.119) | copy-start | bytes 12292
  251.7 60.1 %copy-start.43 = (f32[1024]{0:T(1024)}, f32[1024]{0:T(1024)S(1)}, u32[]{:S(2)}) copy-start(f32[1024]{0:T(1024)S(1)} %convert_element_type.120) | copy-start | bytes 12292
  306.7 29.0 %copy-start.33 = (f32[32,1,128]{2,1,0:T(1,128)}, f32[32,1,128]{2,1,0:T(1,128)S(1)}, u32[]{:S(2)}) copy-start(f32[32,1,128]{2,1,0:T(1,128)S(1)} %convert_element_type.137) | copy-start | bytes 49156
  311.3 39.4 %copy-start.5 = (f32[512,1024]{1,0:T(8,128)}, f32[512,1024]{1,0:T(8,128)S(1)}, u32[]{:S(2)}) copy-start(f32[512,1024]{1,0:T(8,128)S(1)} %get-tuple-element.258) | copy-start | bytes 6291460
  311.3 47.1 %copy-start.22 = (f32[512]{0:T(512)}, f32[512]{0:T(512)S(1)}, u32[]{:S(2)}) copy-start(f32[512]{0:T(512)S(1)} %broadcast_multiply_fusion.4) | copy-start | bytes 6148
  311.7 46.7 %copy-start.35 = (f32[512]{0:T(512)}, f32[512]{0:T(512)S(1)}, u32[]{:S(2)}) copy-start(f32[512]{0:T(512)S(1)} %add_rsqrt_fusion) | copy-start | bytes 6148
  335.7 15.0 %copy-start.47 = (bf16[1024,4096]{1,0:T(8,128)(2,1)S(1)}, bf16[1024,4096]{1,0:T(8,128)(2,1)}, u32[]{:S(2)}) copy-start(bf16[1024,4096]{1,0:T(8,128)(2,1)} %all-gather.10.cloned.1.call-done) | copy-start | bytes 25165828
  361.8 9.2 copy-start.3
  364.2 27.0 %all-to-all-start.1 = ((bf16[512,4,256]{2,0,1:T(8,128)(2,1)}), bf16[512,4,256]{2,0,1:T(8,128)(2,1)}, u32[]{:S(2)}, u32[]{:S(2)}) async-start(bf16[512,4,256]{2,0,1:T(8,128)(2,1)} %bitcast.190), calls=%async_computation.1 | async-start | bytes 2097152 | tf_op jit(solution)/shard_map/all_to_all | solution.py:232
  368.6 414.8 %reduce-scatter.7.cloned.1.call-start = ((), (), s32[]{:S(2)}) async-start(), calls=%async_computation.12 | async-start | bytes 4325376 | tf_op jit(solution)/shard_map/reduce_scatter | solution.py:260
  375.5 456.2 %reduce-scatter.5.cloned.1.call-start = ((), (), s32[]{:S(2)}) async-start(), calls=%async_computation.11 | async-start | bytes 12976128 | tf_op jit(solution)/shard_map/reduce_scatter | solution.py:257
  675.1 345.6 %reduce-scatter.11.cloned.1.call-start = ((), (), s32[]{:S(2)}) async-start(), calls=%async_computation.14 | async-start | bytes 17301504 | tf_op jit(solution)/shard_map/reduce_scatter | solution.py:266
  692.6 515.7 %reduce-scatter.9.cloned.1.call-start = ((), (), s32[]{:S(2)}) async-start(), calls=%async_computation.13 | async-start | bytes 17301504 | tf_op jit(solution)/shard_map/reduce_scatter | solution.py:264
  706.5 13.2 %copy-start.10 = (bf16[512,3,4,256]{0,3,2,1:T(8,128)(2,1)S(1)}, bf16[512,3,4,256]{0,3,2,1:T(8,128)(2,1)}, u32[]{:S(2)}) copy-start(bf16[512,3,4,256]{0,3,2,1:T(8,128)(2,1)} %copy.94) | copy-start | bytes 9437188
  720.1 8.8 copy-start.26
  720.1 8.8 copy-start.27
  720.1 59.7 %copy-start.4 = (f32[512,1024]{1,0:T(8,128)S(1)}, f32[512,1024]{1,0:T(8,128)}, u32[]{:S(2)}) copy-start(f32[512,1024]{1,0:T(8,128)} %copy-done.3) | copy-start | bytes 6291460
  (47 other events, 207.7 us)
Sparse Core Ops, SparseCore 0:
  10.8 70.8 all-gather.5
  84.6 82.9 all-gather.7
  170.4 80.8 all-gather.9
  254.1 81.5 all-gather.11
  375.6 115.2 reduce-scatter.6
  675.2 156.4 reduce-scatter.4
  834.6 186.1 reduce-scatter.10
  1023.6 184.6 reduce-scatter.8
